TPU v7x, 32 devices: a whole 2x2x4 slice. The times are simulated.
32 devices in a mesh: grp: 1, tok: 32 (over z, y, x, core).
Axes of the slice: x: 2, y: 2, z: 4, core: 2. Of those that a mesh axis runs over, the one named last changes fastest.
Arguments:
- queries: bfloat16 [4096, 2048], P(('grp', 'tok')), may hold values from -16 to 16
- keys: bfloat16 [4096, 2048], P(('grp', 'tok')), may hold values from -16 to 16
- values: bfloat16 [4096, 2048], P(('grp', 'tok')), may hold values from -6 to 6
- segment: int32 [4096], P(('grp', 'tok')), may hold values from 0 to 41, never falling along the last dimension, each value on 1 to 256 neighbouring positions
- rates: float32 [4096, 2], P(('grp', 'tok')), may hold values from 0.00046875 to 0.0046875
- fast_one: bfloat16 [2048, 512], P(('grp', 'tok')), may hold values from -0.1875 to 0.1875
- fast_three: bfloat16 [2048, 512], P(('grp', 'tok')), may hold values from -0.1875 to 0.1875
- fast_two: bfloat16 [2048, 512], P(('grp', 'tok')), may hold values from -0.25 to 0.25
Outputs:
- attended: bfloat16 [4096, 2048], P(('grp', 'tok'))
- fast_out: bfloat16 [4096, 2048], P(('grp', 'tok'))
Inputs may be any that keep to these rules, and one draw needn't show every extreme that they name: `segment`: exemplar numbers never fall along the tokens; each exemplar covers 1 to 256 consecutive tokens.
All inputs are finite; a program needn't handle non-finite values.
Results may differ from a plain program's by a relative error of at most 0.0084.
Values may be sent and summed in bfloat16 or wider, within the bound.
A program may use at most 128 MiB of HBM per device.

v0:
```python
import math

import jax
import jax.numpy as jnp
from jax import lax
from jax.sharding import PartitionSpec as P

D = 2048
ATT_HEADS = 16
FAST_HEADS = 2
FAST_DIM = 1024
FAST_HID = 512
WINDOW = 128


EPS = 1e-06


def from_behind(value, axis, steps):
    count = lax.axis_size(axis)
    initial, last = (max(0, -steps), min(count, count - steps))
    return lax.ppermute(value, axis, [(source, source + steps) for source in range(initial, last)])


def project(rows, weight):
    matrix = weight.reshape(FAST_HEADS, FAST_DIM, weight.shape[1])
    return jnp.einsum("thd,hdc->thc", rows, matrix, preferred_element_type=jnp.float32)


def outer_sum(rows, hidden):
    return jnp.einsum("thd,thc->hdc", rows, hidden, preferred_element_type=jnp.float32)


def per_device(queries, keys, values, segment, rates, fast_one, fast_three, fast_two):
    count = queries.shape[0]
    shard = lax.axis_index("tok")
    head_dim = D // ATT_HEADS
    scale = 1.0 / math.sqrt(head_dim)
    seg_low = (segment % 256).astype(jnp.bfloat16)
    prev_keys, prev_values, prev_seg = from_behind((keys, values, seg_low), "tok", 1)
    all_keys = jnp.concatenate([prev_keys, keys], 0)
    all_values = jnp.concatenate([prev_values, values], 0)
    all_seg = jnp.concatenate([prev_seg, seg_low], 0)
    rows = shard * count + jnp.arange(count, dtype=jnp.int32)
    cols = shard * count - count + jnp.arange(2 * count, dtype=jnp.int32)
    allowed = (cols[None, :] <= rows[:, None]) & (rows[:, None] - cols[None, :] < WINDOW)
    allowed = allowed & (cols[None, :] >= 0) & (all_seg[None, :] == seg_low[:, None])
    q_heads = queries.reshape(count, ATT_HEADS, head_dim)
    k_heads = all_keys.reshape(2 * count, ATT_HEADS, head_dim)
    v_heads = all_values.reshape(2 * count, ATT_HEADS, head_dim)
    scores = (
        jnp.einsum("qhd,khd->hqk", q_heads, k_heads, preferred_element_type=jnp.float32) * scale
    )
    masked = jnp.where(allowed[None], scores, jnp.float32(-1e30))
    top = jnp.max(masked, axis=2, keepdims=True)
    expo = jnp.where(allowed[None], jnp.exp(masked - top), jnp.float32(0.0))
    probs = (expo / jnp.sum(expo, axis=2, keepdims=True)).astype(jnp.bfloat16)
    attended = jnp.einsum("hqk,khd->qhd", probs, v_heads, preferred_element_type=jnp.float32)
    attended = attended.reshape(count, D).astype(jnp.bfloat16)
    width = FAST_HEADS * FAST_DIM
    key_fast = keys.reshape(count, FAST_HEADS, FAST_DIM)
    value_fast = values.reshape(count, FAST_HEADS, FAST_DIM)
    query_fast = queries.reshape(count, FAST_HEADS, FAST_DIM)
    full_one, full_three, full_two = (
        lax.all_gather(fast_one, "tok", axis=0, tiled=True),
        lax.all_gather(fast_three, "tok", axis=0, tiled=True),
        lax.all_gather(fast_two, "tok", axis=0, tiled=True),
    )
    rate = rates[:, :, None]
    a_one = project(key_fast, full_one)
    a_three = project(key_fast, full_three)
    sig = jax.nn.sigmoid(a_one)
    weighted = (-rate * a_one * sig * a_three).astype(jnp.bfloat16)
    grad_two = outer_sum(value_fast, weighted).reshape(width, FAST_HID)
    back = -rate * project(value_fast, full_two)
    delta_one = (back * a_three * sig * (1.0 + a_one * (1.0 - sig))).astype(jnp.bfloat16)
    delta_three = (back * a_one * sig).astype(jnp.bfloat16)
    grad_one = outer_sum(key_fast, delta_one).reshape(width, FAST_HID)
    grad_three = outer_sum(key_fast, delta_three).reshape(width, FAST_HID)
    fulls = (full_one, full_three, full_two)
    shares = (
        lax.psum_scatter(grad_one, "tok", scatter_dimension=1, tiled=True),
        lax.psum_scatter(grad_three, "tok", scatter_dimension=1, tiled=True),
        lax.psum_scatter(grad_two, "tok", scatter_dimension=1, tiled=True),
    )
    cols_here = shares[0].shape[1]
    start = shard * cols_here
    fresh = []
    for m in range(3):
        own_cols = lax.dynamic_slice_in_dim(fulls[m], start, cols_here, 1).astype(jnp.float32)
        own_cols = own_cols.reshape(FAST_HEADS, FAST_DIM, cols_here)
        update = own_cols - shares[m].reshape(FAST_HEADS, FAST_DIM, cols_here)
        old_len = jnp.sqrt(jnp.sum(own_cols * own_cols, axis=1))
        new_len = jnp.sqrt(jnp.sum(update * update, axis=1) + EPS)
        scaled = update * (old_len / new_len)[:, None, :]
        fresh.append(scaled.reshape(width, cols_here).astype(jnp.bfloat16))
    new_one, new_three, new_two = (
        lax.all_gather(fresh[0], "tok", axis=1, tiled=True),
        lax.all_gather(fresh[1], "tok", axis=1, tiled=True),
        lax.all_gather(fresh[2], "tok", axis=1, tiled=True),
    )
    b_one = project(query_fast, new_one)
    b_three = project(query_fast, new_three)
    mixed = (jax.nn.silu(b_one) * b_three).astype(jnp.bfloat16)
    down = new_two.reshape(FAST_HEADS, FAST_DIM, FAST_HID)
    fast_out = jnp.einsum("thc,hdc->thd", mixed, down, preferred_element_type=jnp.float32)
    fast_out = fast_out.reshape(count, width).astype(jnp.bfloat16)
    return (attended, fast_out)


def solution(mesh):
    placed = (
        P(("grp", "tok"), None),
        P(("grp", "tok"), None),
        P(("grp", "tok"), None),
        P(("grp", "tok")),
        P(("grp", "tok"), None),
        P(("grp", "tok"), None),
        P(("grp", "tok"), None),
        P(("grp", "tok"), None),
    )
    return jax.shard_map(
        per_device,
        mesh=mesh,
        in_specs=placed,
        out_specs=(P(("grp", "tok"), None), P(("grp", "tok"), None)),
        check_vma=False,
    )
```

profile of v0, /device:TPU:0, one launch (start us, length us, event | category | flops | bytes accessed | tf_op | source)
XLA Modules:
  0.0 811.1 jit_solution(13244500160554908259)
XLA Ops:
  10.1 59.7 %all-gather.9.cloned.1.call-done = bf16[2048,512]{1,0:T(8,128)(2,1)} async-done(((bf16[64,512]{1,0:T(8,128)(2,1)}), bf16[2048,512]{1,0:T(8,128)(2,1)}) %all-gather.9.cloned.1.call-update) | async-done | bytes 2097168 | tf_op jit(solution)/shard_map/all_gather | solution.py:65
  69.8 2.6 convolution_bitcast_fusion.7
  72.4 55.3 %all-gather.11.cloned.1.call-done = bf16[2048,512]{1,0:T(8,128)(2,1)} async-done(((bf16[64,512]{1,0:T(8,128)(2,1)}), bf16[2048,512]{1,0:T(8,128)(2,1)}) %all-gather.11.cloned.1.call-update) | async-done | bytes 2097168 | tf_op jit(solution)/shard_map/all_gather | solution.py:66
  130.3 55.4 %all-gather.7.cloned.1.call-done = bf16[2048,512]{1,0:T(8,128)(2,1)} async-done(((bf16[64,512]{1,0:T(8,128)(2,1)}), bf16[2048,512]{1,0:T(8,128)(2,1)}) %all-gather.7.cloned.1.call-update) | async-done | bytes 2097168 | tf_op jit(solution)/shard_map/all_gather | solution.py:67
  185.7 2.5 fusion.2
  188.2 2.7 convolution_bitcast_fusion.1
  190.9 5.4 copy.92
  196.3 5.4 copy.116
  201.8 2.7 convolution_bitcast_fusion
  204.5 5.4 copy.98
  209.8 5.4 copy.118
  215.4 2.7 convolution_bitcast_fusion.2
  218.0 5.4 copy.86
  223.4 5.4 copy.114
  228.9 114.6 %reduce-scatter.12.cloned.1.call-done = f32[16,2048]{1,0:T(8,128)} async-done(((f32[512,2048]{1,0:T(8,128)}), f32[16,2048]{1,0:T(8,128)}) %reduce-scatter.12.cloned.1.call-update) | async-done | bytes 131088
  348.4 136.0 %reduce-scatter.14.cloned.1.call-done = f32[16,2048]{1,0:T(8,128)} async-done(((f32[512,2048]{1,0:T(8,128)}), f32[16,2048]{1,0:T(8,128)}) %reduce-scatter.14.cloned.1.call-update) | async-done | bytes 131088
  489.2 135.9 %reduce-scatter.10.cloned.1.call-done = f32[16,2048]{1,0:T(8,128)} async-done(((f32[512,2048]{1,0:T(8,128)}), f32[16,2048]{1,0:T(8,128)}) %reduce-scatter.10.cloned.1.call-update) | async-done | bytes 131088
  642.4 37.8 %all-gather.15.cloned.1.call-done = bf16[2048,512]{0,1:T(8,128)(2,1)} async-done(((bf16[2048,16]{0,1:T(8,128)(2,1)}), bf16[2048,512]{0,1:T(8,128)(2,1)}) %all-gather.15.cloned.1.call-update) | async-done | bytes 2097168 | tf_op jit(solution)/shard_map/all_gather | solution.py:98
  680.2 2.9 copy.94
  683.0 55.6 %all-gather.17.cloned.1.call-done = bf16[2048,512]{0,1:T(8,128)(2,1)} async-done(((bf16[2048,16]{0,1:T(8,128)(2,1)}), bf16[2048,512]{0,1:T(8,128)(2,1)}) %all-gather.17.cloned.1.call-update) | async-done | bytes 2097168 | tf_op jit(solution)/shard_map/all_gather | solution.py:99
  738.7 3.9 copy.100
  744.3 52.3 %all-gather.13.cloned.1.call-done = bf16[2048,512]{0,1:T(8,128)(2,1)} async-done(((bf16[2048,16]{0,1:T(8,128)(2,1)}), bf16[2048,512]{0,1:T(8,128)(2,1)}) %all-gather.13.cloned.1.call-update) | async-done | bytes 2097168 | tf_op jit(solution)/shard_map/all_gather | solution.py:100
  796.6 3.9 copy.88
  800.5 3.0 convolution_convert_fusion
  (66 shorter events, 35.1 us)
Async XLA Ops:
  7.2 120.6 %copy-start = (bf16[128,2048]{1,0:T(8,128)(2,1)S(1)}, bf16[128,2048]{1,0:T(8,128)(2,1)}, u32[]{:S(2)}) copy-start(bf16[128,2048]{1,0:T(8,128)(2,1)} %param.9) | copy-start | bytes 1572868
  7.2 62.6 %all-gather.9.cloned.1.call-start = ((), (), s32[]{:S(2)}) async-start(), calls=%async_computation.4 | async-start | bytes 2162688 | tf_op jit(solution)/shard_map/all_gather | solution.py:65
  7.9 119.8 %all-gather.11.cloned.1.call-start = ((), (), s32[]{:S(2)}) async-start(), calls=%async_computation.5 | async-start | bytes 2162688 | tf_op jit(solution)/shard_map/all_gather | solution.py:66
  8.7 177.0 %all-gather.7.cloned.1.call-start = ((), (), s32[]{:S(2)}) async-start(), calls=%async_computation.3 | async-start | bytes 2162688 | tf_op jit(solution)/shard_map/all_gather | solution.py:67
  9.4 334.1 %reduce-scatter.12.cloned.1.call-start = ((), (), s32[]{:S(2)}) async-start(), calls=%async_computation.10 | async-start | bytes 4325376
  72.4 113.3 %copy-start.1 = (bf16[128,2048]{1,0:T(8,128)(2,1)S(1)}, bf16[128,2048]{1,0:T(8,128)(2,1)}, u32[]{:S(2)}) copy-start(bf16[128,2048]{1,0:T(8,128)(2,1)} %param.10) | copy-start | bytes 1572868
  201.7 282.7 %reduce-scatter.14.cloned.1.call-start = ((), (), s32[]{:S(2)}) async-start(), calls=%async_computation.11 | async-start | bytes 4325376
  215.3 409.8 %reduce-scatter.10.cloned.1.call-start = ((), (), s32[]{:S(2)}) async-start(), calls=%async_computation.9 | async-start | bytes 4325376
  228.8 451.3 %all-gather.15.cloned.1.call-start = ((), (), s32[]{:S(2)}) async-start(), calls=%async_computation.7 | async-start | bytes 2162688 | tf_op jit(solution)/shard_map/all_gather | solution.py:98
  348.3 390.4 %all-gather.17.cloned.1.call-start = ((), (), s32[]{:S(2)}) async-start(), calls=%async_computation.8 | async-start | bytes 2162688 | tf_op jit(solution)/shard_map/all_gather | solution.py:99
  489.2 307.4 %all-gather.13.cloned.1.call-start = ((), (), s32[]{:S(2)}) async-start(), calls=%async_computation.6 | async-start | bytes 2162688 | tf_op jit(solution)/shard_map/all_gather | solution.py:100
  626.4 4.9 copy-start.4
  630.0 5.3 collective-permute-start
  631.3 3.7 collective-permute-start.1
  632.9 3.0 collective-permute-start.2
  635.3 1.7 copy-start.3
  744.3 56.2 %copy-start.2 = (bf16[2048,512]{1,0:T(8,128)(2,1)S(1)}, bf16[2048,512]{1,0:T(8,128)(2,1)}, u32[]{:S(2)}) copy-start(bf16[2048,512]{1,0:T(8,128)(2,1)} %copy.100) | copy-start | bytes 6291460
Sparse Core Ops, SparseCore 0:
  10.8 58.9 all-gather.8
  72.7 55.0 all-gather.10
  130.6 55.0 all-gather.6
  201.8 141.6 reduce-scatter.11
  345.6 138.7 reduce-scatter.13
  486.5 138.5 reduce-scatter.9
  628.0 52.1 all-gather.14
  683.6 55.0 all-gather.16
  741.5 55.0 all-gather.12
where the time goes:
time: 812 us; the launch traced here: 811 us
  waiting for transfers between devices  705 us (87%)
  local copies, waits for them, and re-layouts  52.1 us (6%)
  matrix products  24.7 us (3%)
  between operations  14.1 us (2%)
  other arithmetic  10.3 us (1%)
    unnamed x12, waiting for transfers between devices  389 us
    all_gather x1, waiting for transfers between devices, per_device(): lax.all_gather(fast_one, 'tok', axis=0, tiled=True)  59.7 us
    all_gather x1, waiting for transfers between devices, per_device(): lax.all_gather(fresh[1], 'tok', axis=1, tiled=True)  55.6 us
    all_gather x1, waiting for transfers between devices, per_device(): lax.all_gather(fast_two, 'tok', axis=0, tiled=True)  55.4 us
    all_gather x1, waiting for transfers between devices, per_device(): lax.all_gather(fast_three, 'tok', axis=0, tiled=True)  55.3 us
    all_gather x1, waiting for transfers between devices, per_device(): lax.all_gather(fresh[2], 'tok', axis=1, tiled=True)  52.3 us
    all_gather x1, waiting for transfers between devices, per_device(): lax.all_gather(fresh[0], 'tok', axis=1, tiled=True)  37.8 us
    unnamed x19, local copies, waits for them, and re-layouts  22.2 us
  transfers between devices with their start and end apart: 12, of which 9 were waited for; matrix products, arithmetic and copies ran while one was open for 8% of the time, Pallas kernels for 0%

commit v1 on v0

v1 whole, which is shorter than its diff:
```python
import functools
import math

import jax
import jax.numpy as jnp
from jax import lax
from jax.experimental import pallas as pl
from jax.experimental.pallas import tpu as pltpu
from jax.sharding import PartitionSpec as P

D = 2048
ATT_HEADS = 16
FAST_HEADS = 2
FAST_DIM = 1024
FAST_HID = 512
WINDOW = 128


EPS = 1e-06


def from_behind(value, axis, steps):
    count = lax.axis_size(axis)
    initial, last = (max(0, -steps), min(count, count - steps))
    return lax.ppermute(value, axis, [(source, source + steps) for source in range(initial, last)])


def axis_orders(count):
    bits = count.bit_length() - 1
    rest = list(range(1, bits))
    return [[0] + rest[m:] + rest[:m] if rest else [0] for m in range(3)]


def bit_of(index, bit):
    return lax.rem(lax.div(index, jnp.int32(1 << bit)), jnp.int32(2))


def block_of(index, order):
    total = jnp.int32(0)
    for bit in order:
        total = total * 2 + bit_of(index, bit)
    return total


def device_of(block, order):
    index = 0
    for place, bit in enumerate(reversed(order)):
        index += ((block >> place) & 1) << bit
    return index


def greet(me, bits):
    barrier = pltpu.get_barrier_semaphore()
    for bit in range(bits):
        pl.semaphore_signal(
            barrier,
            inc=1,
            device_id={"tok": partner_of(me, bit)},
            device_id_type=pl.DeviceIdType.MESH,
        )
    pl.semaphore_wait(barrier, bits)


def partner_of(me, bit):
    return me + (1 - 2 * bit_of(me, bit)) * (1 << bit)


def remote(src, dst, send_sem, recv_sem, partner):
    return pltpu.make_async_remote_copy(
        src_ref=src,
        dst_ref=dst,
        send_sem=send_sem,
        recv_sem=recv_sem,
        device_id={"tok": partner},
        device_id_type=pl.DeviceIdType.MESH,
    )


def gather_kernel(count, *refs):
    orders = axis_orders(count)
    bits = count.bit_length() - 1
    parts, outs = refs[:3], refs[3:6]
    held, local_sem, send_sem, recv_sem = refs[6:]
    me = lax.axis_index("tok")
    own = [block_of(me, orders[m]) for m in range(3)]
    local = [
        pltpu.make_async_copy(parts[m], held.at[m, own[m]], local_sem.at[m]) for m in range(3)
    ]
    for copy in local:
        copy.start()
    greet(me, bits)
    copies = {}

    def send(m, step):
        bit = orders[m][bits - 1 - step]
        size = 1 << step
        start = lax.div(own[m], jnp.int32(size)) * size
        here = held.at[m, pl.ds(start, size)]
        copies[m, step] = remote(
            here, here, send_sem.at[m, step], recv_sem.at[m, step], partner_of(me, bit)
        )
        copies[m, step].start()

    for m in range(3):
        local[m].wait()
        send(m, 0)
    for step in range(bits):
        for m in range(3):
            copies[m, step].wait_recv()
            if step + 1 < bits:
                send(m, step + 1)
            else:
                for block in range(count):
                    outs[m][device_of(block, orders[m])] = held[m, block]
    for copy in copies.values():
        copy.wait_send()


def gather_weights(weights, count):
    rows, cols = weights[0].shape
    bits = count.bit_length() - 1
    outs = pl.pallas_call(
        functools.partial(gather_kernel, count),
        out_shape=[jax.ShapeDtypeStruct((count, rows, cols), jnp.bfloat16)] * 3,
        in_specs=[pl.BlockSpec(memory_space=pltpu.VMEM)] * 3,
        out_specs=[pl.BlockSpec(memory_space=pltpu.VMEM)] * 3,
        scratch_shapes=[
            pltpu.VMEM((3, count, rows, cols), jnp.bfloat16),
            pltpu.SemaphoreType.DMA((3,)),
            pltpu.SemaphoreType.DMA((3, bits)),
            pltpu.SemaphoreType.DMA((3, bits)),
        ],
        compiler_params=pltpu.CompilerParams(collective_id=0, has_side_effects=True),
        cost_estimate=pl.CostEstimate(flops=0, bytes_accessed=100_000_000, transcendentals=0),
    )(*weights)
    return [out.reshape(count * rows, cols) for out in outs]


def update_kernel(count, *refs):
    orders = axis_orders(count)
    bits = count.bit_length() - 1
    grads, olds, outs = refs[:3], refs[3:6], refs[6:9]
    total, landed, send_sem, recv_sem = refs[9:]
    me = lax.axis_index("tok")
    own = [block_of(me, orders[m]) for m in range(3)]
    greet(me, bits)
    copies = {}

    def first_kept(m, step):
        size = count >> (step + 1)
        return lax.div(own[m], jnp.int32(size)) * size

    def half_start(m):
        return lax.div(own[m], jnp.int32(count // 2)) * (count // 2)

    def send_half(m, step):
        bit = orders[m][step]
        size = count >> (step + 1)
        keep = first_kept(m, step)
        away = keep + (1 - 2 * bit_of(me, bit)) * size
        if step == 0:
            src = grads[m].at[pl.ds(away, size)]
        else:
            src = total.at[m, pl.ds(away - half_start(m), size)]
        dst = landed.at[m, pl.ds(count - 2 * size, size)]
        copies[m, step] = remote(
            src, dst, send_sem.at[m, step], recv_sem.at[m, step], partner_of(me, bit)
        )
        copies[m, step].start()

    def send_new(m, step):
        bit = orders[m][bits - 1 - step]
        size = 1 << step
        start = lax.div(own[m], jnp.int32(size)) * size
        here = outs[m].at[pl.ds(start, size)]
        at = bits + step
        copies[m, at] = remote(
            here, here, send_sem.at[m, at], recv_sem.at[m, at], partner_of(me, bit)
        )
        copies[m, at].start()

    def add_half(m, step):
        size = count >> (step + 1)
        keep = first_kept(m, step)
        offset = keep - half_start(m)

        def one(i, carry):
            mine = grads[m][keep + i] if step == 0 else total[m, offset + i]
            other = landed[m, count - 2 * size + i]
            both = mine.astype(jnp.float32) + other.astype(jnp.float32)
            total[m, offset + i] = both.astype(jnp.bfloat16)
            return carry

        lax.fori_loop(0, size, one, 0)

    for m in range(3):
        send_half(m, 0)
    for step in range(bits - 1):
        for m in range(3):
            copies[m, step].wait_recv()
            add_half(m, step)
            send_half(m, step + 1)
    for m in range(3):
        copies[m, bits - 1].wait_recv()
        mine = total[m, own[m] - half_start(m)] if bits > 1 else grads[m][own[m]]
        grad = mine.astype(jnp.float32) + landed[m, count - 2].astype(jnp.float32)
        old = olds[m][...].astype(jnp.float32)
        update = old - grad
        old_len = jnp.sqrt(jnp.sum(old * old, axis=1, keepdims=True))
        new_len = jnp.sqrt(jnp.sum(update * update, axis=1, keepdims=True) + EPS)
        outs[m][own[m]] = (update * (old_len / new_len)).astype(jnp.bfloat16)
        send_new(m, 0)
    for step in range(bits):
        for m in range(3):
            copies[m, bits + step].wait_recv()
            if step + 1 < bits:
                send_new(m, step + 1)
    for copy in copies.values():
        copy.wait_send()


def update_weights(grads, olds, count):
    rows, cols = olds[0].shape
    bits = count.bit_length() - 1
    shape = (count, rows, cols)
    return pl.pallas_call(
        functools.partial(update_kernel, count),
        out_shape=[jax.ShapeDtypeStruct(shape, jnp.bfloat16)] * 3,
        in_specs=[pl.BlockSpec(memory_space=pltpu.VMEM)] * 6,
        out_specs=[pl.BlockSpec(memory_space=pltpu.VMEM)] * 3,
        scratch_shapes=[
            pltpu.VMEM((3, count // 2, rows, cols), jnp.bfloat16),
            pltpu.VMEM((3, count, rows, cols), jnp.bfloat16),
            pltpu.SemaphoreType.DMA((3, 2 * bits)),
            pltpu.SemaphoreType.DMA((3, 2 * bits)),
        ],
        compiler_params=pltpu.CompilerParams(collective_id=1, has_side_effects=True),
        cost_estimate=pl.CostEstimate(flops=0, bytes_accessed=200_000_000, transcendentals=0),
    )(*[grad.reshape(shape) for grad in grads], *olds)


def project(rows, weight):
    matrix = weight.reshape(FAST_HEADS, FAST_DIM, weight.shape[1])
    return jnp.einsum("thd,hdc->thc", rows, matrix, preferred_element_type=jnp.float32)


def outer_sum(hidden, rows):
    summed = jnp.einsum("thc,thd->hcd", hidden, rows, preferred_element_type=jnp.float32)
    return summed.astype(jnp.bfloat16).reshape(FAST_HEADS * FAST_HID, FAST_DIM)


def per_device(queries, keys, values, segment, rates, fast_one, fast_three, fast_two):
    count = queries.shape[0]
    devices = lax.axis_size("tok")
    shard = lax.axis_index("tok")
    head_dim = D // ATT_HEADS
    scale = 1.0 / math.sqrt(head_dim)
    seg_low = (segment % 256).astype(jnp.bfloat16)
    prev_keys, prev_values, prev_seg = from_behind((keys, values, seg_low), "tok", 1)
    all_keys = jnp.concatenate([prev_keys, keys], 0)
    all_values = jnp.concatenate([prev_values, values], 0)
    all_seg = jnp.concatenate([prev_seg, seg_low], 0)
    rows = shard * count + jnp.arange(count, dtype=jnp.int32)
    cols = shard * count - count + jnp.arange(2 * count, dtype=jnp.int32)
    allowed = (cols[None, :] <= rows[:, None]) & (rows[:, None] - cols[None, :] < WINDOW)
    allowed = allowed & (cols[None, :] >= 0) & (all_seg[None, :] == seg_low[:, None])
    q_heads = queries.reshape(count, ATT_HEADS, head_dim)
    k_heads = all_keys.reshape(2 * count, ATT_HEADS, head_dim)
    v_heads = all_values.reshape(2 * count, ATT_HEADS, head_dim)
    scores = (
        jnp.einsum("qhd,khd->hqk", q_heads, k_heads, preferred_element_type=jnp.float32) * scale
    )
    masked = jnp.where(allowed[None], scores, jnp.float32(-1e30))
    top = jnp.max(masked, axis=2, keepdims=True)
    expo = jnp.where(allowed[None], jnp.exp(masked - top), jnp.float32(0.0))
    probs = (expo / jnp.sum(expo, axis=2, keepdims=True)).astype(jnp.bfloat16)
    attended = jnp.einsum("hqk,khd->qhd", probs, v_heads, preferred_element_type=jnp.float32)
    attended = attended.reshape(count, D).astype(jnp.bfloat16)
    width = FAST_HEADS * FAST_DIM
    key_fast = keys.reshape(count, FAST_HEADS, FAST_DIM)
    value_fast = values.reshape(count, FAST_HEADS, FAST_DIM)
    query_fast = queries.reshape(count, FAST_HEADS, FAST_DIM)
    fulls = gather_weights((fast_one, fast_three, fast_two), devices)
    full_one, full_three, full_two = fulls
    rate = rates[:, :, None]
    a_one = project(key_fast, full_one)
    a_three = project(key_fast, full_three)
    sig = jax.nn.sigmoid(a_one)
    weighted = (-rate * a_one * sig * a_three).astype(jnp.bfloat16)
    back = -rate * project(value_fast, full_two)
    delta_one = (back * a_three * sig * (1.0 + a_one * (1.0 - sig))).astype(jnp.bfloat16)
    delta_three = (back * a_one * sig).astype(jnp.bfloat16)
    grads = (
        outer_sum(delta_one, key_fast),
        outer_sum(delta_three, key_fast),
        outer_sum(weighted, value_fast),
    )
    rows_here = FAST_HEADS * FAST_HID // devices
    olds = []
    for m, order in enumerate(axis_orders(devices)):
        start = block_of(shard, order) * rows_here
        own_cols = lax.dynamic_slice(
            fulls[m].reshape(FAST_HEADS, FAST_DIM, FAST_HID),
            (start // FAST_HID, jnp.int32(0), start % FAST_HID),
            (1, FAST_DIM, rows_here),
        )
        olds.append(own_cols[0].T)
    news = update_weights(grads, olds, devices)
    new_one, new_three, new_two = [n.reshape(FAST_HEADS, FAST_HID, FAST_DIM) for n in news]
    b_one = jnp.einsum("thd,hcd->thc", query_fast, new_one, preferred_element_type=jnp.float32)
    b_three = jnp.einsum("thd,hcd->thc", query_fast, new_three, preferred_element_type=jnp.float32)
    mixed = (jax.nn.silu(b_one) * b_three).astype(jnp.bfloat16)
    fast_out = jnp.einsum("thc,hcd->thd", mixed, new_two, preferred_element_type=jnp.float32)
    fast_out = fast_out.reshape(count, width).astype(jnp.bfloat16)
    return (attended, fast_out)


def solution(mesh):
    placed = (
        P(("grp", "tok"), None),
        P(("grp", "tok"), None),
        P(("grp", "tok"), None),
        P(("grp", "tok")),
        P(("grp", "tok"), None),
        P(("grp", "tok"), None),
        P(("grp", "tok"), None),
        P(("grp", "tok"), None),
    )
    return jax.shard_map(
        per_device,
        mesh=mesh,
        in_specs=placed,
        out_specs=(P(("grp", "tok"), None), P(("grp", "tok"), None)),
        check_vma=False,
    )
```

time: 812 us -> 184 us (0.23)
  waiting for transfers between devices: 705 us -> 0.01 us
  Pallas kernels: 0 us -> 137 us
  local copies, waits for them, and re-layouts: 52.1 us -> 11.2 us
  between operations: 14.1 us -> 0.88 us
    unnamed x12 -> x0, waiting for transfers between devices: 389 us -> none
    all_gather x6 -> x0, waiting for transfers between devices: 316 us -> none  [the longest x1 59.7 us: per_device(): lax.all_gather(fast_one, 'tok', axis=0, tiled=True)]
    pallas_call x0 -> x2, Pallas kernels: none -> 137 us  [the longest x1 87 us: update_weights(): pl.pallas_call(functools.partial(update_kernel, count), out_shape=[jax.Sh...]
    dot_general x3 -> x0, local copies, waits for them, and re-layouts: 16.2 us -> none  [outer_sum(): jnp.einsum('thd,thc->hdc', rows, hidden, preferred_element_type=jnp.float32)]
    unnamed x19 -> x18, local copies, waits for them, and re-layouts: 22.2 us -> 7.11 us
    all_gather x3 -> x0, local copies, waits for them, and re-layouts: 10.7 us -> none  [the longest x1 3.92 us: per_device(): lax.all_gather(fresh[1], 'tok', axis=1, tiled=True)]
  transfers between devices with their start and end apart: 12 -> 3, of which waited for: 9 -> 0; matrix products, arithmetic and copies ran while one was open for 8% -> 15% of each run, Pallas kernels for 0% -> 75%
where the time goes in v1:
time: 184 us; the launch traced here: 183 us
  Pallas kernels  137 us (74%)
  matrix products  21.1 us (11%)
  local copies, waits for them, and re-layouts  11.2 us (6%)
  starting transfers between devices  9.93 us (5%)
  other arithmetic  3.38 us (2%)
    pallas_call x1, Pallas kernels, update_weights(): pl.pallas_call(functools.partial(update_kernel, count), out_shape=[jax.Sh...  87 us
    pallas_call x1, Pallas kernels, gather_weights(): pl.pallas_call(functools.partial(gather_kernel, count), out_shape=[jax.Sh...  49.9 us
    ppermute x3, starting transfers between devices, from_behind(): lax.ppermute(value, axis, [(source, source + steps) for source in range(i...  9.93 us
    unnamed x18, local copies, waits for them, and re-layouts  7.11 us
    dot_general x3, matrix products, outer_sum(): jnp.einsum('thc,thd->hcd', hidden, rows, preferred_element_type=jnp.float32)  6.17 us
    dot_general x3, matrix products, project(): jnp.einsum('thd,hdc->thc', rows, matrix, preferred_element_type=jnp.float32)  4.66 us
  transfers between devices with their start and end apart: 3, of which 0 were waited for; matrix products, arithmetic and copies ran while one was open for 15% of the time, Pallas kernels for 75%

profile of v1, /device:TPU:0, one launch (start us, length us, event | category | flops | bytes accessed | tf_op | source)
XLA Modules:
  0.0 183.4 jit_solution(8005891371663829103)
XLA Ops:
  1.3 2.5 %collective-permute-start.1 = (bf16[128]{0:T(256)(128)(2,1)S(1)}, bf16[128]{0:T(256)(128)(2,1)S(1)}, u32[]{:S(2)}, u32[]{:S(2)}) collective-permute-start(bf16[128]{0:T(256)(128)(2,1)S(1)} %fusion.40), channel_id=1, source_target_pairs={{0,1},{1,2},{2,3},{3,4},{4,5},{5,6},{6,7},{7,8},{8,9},{9,10},{10,1... | collective-permute-start | bytes 776 | tf_op jit(solution)/shard_map/ppermute | solution.py:25
  3.8 2.0 %copy.31 = bf16[128,2048]{0,1:T(8,128)(2,1)} copy(bf16[128,2048]{1,0:T(8,128)(2,1)} %param.9) | data formatting | bytes 1048576 | tf_op args[1]
  5.9 5.3 %collective-permute-start.2 = (bf16[128,2048]{0,1:T(8,128)(2,1)}, bf16[128,2048]{0,1:T(8,128)(2,1)}, u32[]{:S(2)}, u32[]{:S(2)}) collective-permute-start(bf16[128,2048]{0,1:T(8,128)(2,1)} %copy.31), channel_id=1, source_target_pairs={{0,1},{1,2},{2,3},{3,4},{4,5},{5,6},{6,7},{7,8},{8,9},{9,10},{10,1... | collective-permute-start | bytes 1572872 | tf_op jit(solution)/shard_map/ppermute | solution.py:25
  11.2 2.1 %collective-permute-start = (bf16[128,2048]{1,0:T(8,128)(2,1)}, bf16[128,2048]{1,0:T(8,128)(2,1)}, u32[]{:S(2)}, u32[]{:S(2)}) collective-permute-start(bf16[128,2048]{1,0:T(8,128)(2,1)} %param.10), channel_id=1, source_target_pairs={{0,1},{1,2},{2,3},{3,4},{4,5},{5,6},{6,7},{7,8},{8,9},{9,10},{10,1... | collective-permute-start | bytes 1572872 | tf_op jit(solution)/shard_map/ppermute | solution.py:25
  13.3 49.9 %shard_map.95 = (bf16[32,64,512]{2,1,0:T(8,128)(2,1)}, bf16[32,64,512]{2,1,0:T(8,128)(2,1)}, bf16[32,64,512]{2,1,0:T(8,128)(2,1)}) custom-call(bf16[64,512]{1,0:T(8,128)(2,1)} %refs_0_.1, bf16[64,512]{1,0:T(8,128)(2,1)} %refs_1_.1, bf16[64,512]{1,0:T(8,128)(2,1)} %refs_2_.1), custom_call_target="tpu_custom_call" | custom-call | bytes 100000000 | tf_op jit(solution)/shard_map/pallas_call | solution.py:122
  63.2 2.7 %convolution_bitcast_fusion.2 = f32[128,2,512]{0,2,1:T(8,128)S(1)} fusion(bf16[2,1024,512]{2,1,0:T(8,128)(2,1)} %bitcast.103, bf16[16,2,8,1024]{3,2,1,0:T(8,128)(2,1)} %bitcast.94), kind=kOutput, calls=%fused_computation.12 | convolution fusion | flops 268435456 | bytes 3145728 | tf_op jit(solution)/shard_map/thd,hdc->thc/dot_general | solution.py:244
  66.0 1.0 convolution_bitcast_fusion.3
  67.7 1.0 fusion.2
  68.7 2.0 %convolution_convert_fusion.1 = bf16[2,512,1024]{2,1,0:T(8,128)(2,1)} fusion(bf16[16,2,8,1024]{3,2,1,0:T(8,128)(2,1)S(1)} %bitcast.96, f32[128,2,512]{0,2,1:T(8,128)S(1)} %fusion.2, f32[128,2,512]{0,2,1:T(8,128)S(1)} %convolution_bitcast_fusion.2), kind=kOutput, calls=%fused_computation.5 | convolution fusion | flops 270270464 | bytes 3670016 | tf_op jit(solution)/shard_map/thc,thd->hcd/dot_general | solution.py:248
  70.8 2.1 %convolution_convert_fusion.2 = bf16[2,512,1024]{2,1,0:T(8,128)(2,1)} fusion(bf16[16,2,8,1024]{3,2,1,0:T(8,128)(2,1)S(1)} %bitcast.97, f32[128,2,512]{0,2,1:T(8,128)S(1)} %convolution_bitcast_fusion.2, f32[128,2,512]{0,2,1:T(8,128)S(1)} %fusion.2, f32[128,2,512]{0,2,1:T(8,128)S(1)} %convolution_bitcast_fusion.3), kind=kOutput, calls=%fused_computation.6 | convolution fusion | flops 270794752 | bytes 4194304 | tf_op jit(solution)/shard_map/thc,thd->hcd/dot_general | solution.py:248
  72.8 2.0 %convolution_convert_fusion = bf16[2,512,1024]{2,1,0:T(8,128)(2,1)} fusion(bf16[16,2,8,1024]{3,2,1,0:T(8,128)(2,1)S(1)} %bitcast.102, f32[128,2,512]{0,2,1:T(8,128)S(1)} %convolution_bitcast_fusion.3, f32[128,2,512]{0,2,1:T(8,128)S(1)} %convolution_bitcast_fusion.2, f32[128,2]{0,1:T(2,128)S(1)} %neg.12), kind=kOutput, calls=%fused_computation.4 | convolution fusion | flops 270401536 | bytes 3671040 | tf_op jit(solution)/shard_map/thc,thd->hcd/dot_general | solution.py:248
  74.9 1.1 constant_dynamic-slice_fusion
  76.0 0.8 copy.63
  77.6 1.1 constant_dynamic-slice_fusion.2
  79.5 1.3 copy.64
  80.8 87.0 %shard_map.96 = (bf16[32,32,1024]{2,1,0:T(8,128)(2,1)}, bf16[32,32,1024]{2,1,0:T(8,128)(2,1)}, bf16[32,32,1024]{2,1,0:T(8,128)(2,1)}) custom-call(bf16[32,32,1024]{2,1,0:T(8,128)(2,1)} %bitcast.99, bf16[32,32,1024]{2,1,0:T(8,128)(2,1)} %bitcast.98, bf16[32,32,1024]{2,1,0:T(8,128)(2,1)} %bitcast.100, bf16[32,1024]{1,0:T(8,128)(2,1)} %bitcast.118, ...), custom_call_target="tpu_custom_call" | custom-call | bytes 200000000 | tf_op jit(solution)/shard_map/pallas_call | solution.py:226
  167.8 2.3 %convolution_bitcast_fusion.1 = f32[128,2,512]{0,2,1:T(8,128)S(1)} fusion(bf16[2,512,1024]{2,1,0:T(8,128)(2,1)} %bitcast.109, bf16[128,2,1024]{0,2,1:T(8,128)(2,1)S(1)} %bitcast.110), kind=kOutput, calls=%fused_computation.11 | convolution fusion | flops 268435456 | bytes 3145728 | tf_op jit(solution)/shard_map/thd,hcd->thc/dot_general | solution.py:310
  170.1 3.6 %convolution_convert_fusion.3 = bf16[2,1024,128]{2,1,0:T(8,128)(2,1)S(1)} fusion(bf16[2,512,1024]{2,1,0:T(8,128)(2,1)} %bitcast.120, bf16[2,512,1024]{2,1,0:T(8,128)(2,1)} %bitcast.119, bf16[128,2,1024]{0,2,1:T(8,128)(2,1)S(1)} %bitcast.111, f32[128,2,512]{0,2,1:T(8,128)S(1)} %convolution_bitcast_fusion.1), kind=kOutput, calls=%fused_computation.8 | convolution fusion | flops 537919488 | bytes 5767168 | tf_op jit(solution)/shard_map/thc,hcd->thd/dot_general | solution.py:313
  173.7 1.0 copy.52
  174.9 1.2 pad_maximum_fusion
  176.7 1.3 pad_maximum_fusion.1
  178.0 2.3 %fusion.50 = (f32[16,128]{1,0:T(8,128)S(1)}, f32[16,128,256]{1,2,0:T(8,128)}) fusion(pred[128,256]{0,1:T(8,128)(4,1)S(1)} %fusion.35, bf16[256,16,128]{0,2,1:T(8,128)(2,1)S(1)} %bitcast.113, bf16[128,2048]{1,0:T(8,128)(2,1)S(1)} %copy-done.4), kind=kOutput, calls=%fused_computation.74 | convolution fusion | flops 136839424 | bytes 3710976 | tf_op jit(solution)/shard_map/sub | solution.py:275
  180.3 2.0 %convolution_convert_fusion.4 = bf16[16,128,128]{2,1,0:T(8,128)(2,1)S(1)} fusion(bf16[256,16,128]{0,2,1:T(8,128)(2,1)S(1)} %bitcast.112, f32[16,128,256]{1,2,0:T(8,128)} %get-tuple-element.19, f32[16,128]{1,0:T(8,128)S(1)} %get-tuple-element.18), kind=kOutput, calls=%fused_computation.9 | convolution fusion | flops 135528448 | bytes 3678208 | tf_op jit(solution)/shard_map/hqk,khd->qhd/dot_general | solution.py:277
  182.4 1.0 copy.51
  (26 shorter events, 3.8 us)
Async XLA Ops:
  1.3 64.7 %copy-start = (bf16[128,2048]{1,0:T(8,128)(2,1)S(1)}, bf16[128,2048]{1,0:T(8,128)(2,1)}, u32[]{:S(2)}) copy-start(bf16[128,2048]{1,0:T(8,128)(2,1)} %param.9) | copy-start | bytes 1572868
  1.3 173.4 %collective-permute-start.1 = (bf16[128]{0:T(256)(128)(2,1)S(1)}, bf16[128]{0:T(256)(128)(2,1)S(1)}, u32[]{:S(2)}, u32[]{:S(2)}) collective-permute-start(bf16[128]{0:T(256)(128)(2,1)S(1)} %fusion.40), channel_id=1, source_target_pairs={{0,1},{1,2},{2,3},{3,4},{4,5},{5,6},{6,7},{7,8},{8,9},{9,10},{10,1... | collective-permute-start | bytes 776 | tf_op jit(solution)/shard_map/ppermute | solution.py:25
  5.9 170.8 %collective-permute-start.2 = (bf16[128,2048]{0,1:T(8,128)(2,1)}, bf16[128,2048]{0,1:T(8,128)(2,1)}, u32[]{:S(2)}, u32[]{:S(2)}) collective-permute-start(bf16[128,2048]{0,1:T(8,128)(2,1)} %copy.31), channel_id=1, source_target_pairs={{0,1},{1,2},{2,3},{3,4},{4,5},{5,6},{6,7},{7,8},{8,9},{9,10},{10,1... | collective-permute-start | bytes 1572872 | tf_op jit(solution)/shard_map/ppermute | solution.py:25
  11.2 163.7 %collective-permute-start = (bf16[128,2048]{1,0:T(8,128)(2,1)}, bf16[128,2048]{1,0:T(8,128)(2,1)}, u32[]{:S(2)}, u32[]{:S(2)}) collective-permute-start(bf16[128,2048]{1,0:T(8,128)(2,1)} %param.10), channel_id=1, source_target_pairs={{0,1},{1,2},{2,3},{3,4},{4,5},{5,6},{6,7},{7,8},{8,9},{9,10},{10,1... | collective-permute-start | bytes 1572872 | tf_op jit(solution)/shard_map/ppermute | solution.py:25
  63.2 2.8 %copy-start.2 = (bf16[32,64,512]{2,1,0:T(8,128)(2,1)S(1)}, bf16[32,64,512]{2,1,0:T(8,128)(2,1)}, u32[]{:S(2)}) copy-start(bf16[32,64,512]{2,1,0:T(8,128)(2,1)} %get-tuple-element.9) | copy-start | bytes 6291460
  66.0 1.0 copy-start.5
  66.0 1.1 copy-start.1
  66.0 1.8 copy-start.3
  176.1 1.9 %copy-start.4 = (bf16[128,2048]{1,0:T(8,128)(2,1)S(1)}, bf16[128,2048]{1,0:T(8,128)(2,1)}, u32[]{:S(2)}) copy-start(bf16[128,2048]{1,0:T(8,128)(2,1)} %param.8) | copy-start | bytes 1572868

commit v2 on v1

v2 whole, which is shorter than its diff:
```python
import functools
import math

import jax
import jax.numpy as jnp
from jax import lax
from jax.experimental import pallas as pl
from jax.experimental.pallas import tpu as pltpu
from jax.sharding import PartitionSpec as P

D = 2048
ATT_HEADS = 16
FAST_HEADS = 2
FAST_DIM = 1024
FAST_HID = 512
WINDOW = 128


EPS = 1e-06


def axis_orders(count):
    bits = count.bit_length() - 1
    rest = list(range(1, bits))
    return [[0] + rest[m:] + rest[:m] if rest else [0] for m in range(3)]


def bit_of(index, bit):
    return lax.rem(lax.div(index, jnp.int32(1 << bit)), jnp.int32(2))


def coordinate(index, bit, bits):
    here = bit_of(index, bit)
    if bits >= 3 and bit == bits - 2:
        top = bit_of(index, bits - 1)
        here = here + top - 2 * here * top
    return here


def partner_of(me, bit, bits):
    other = me + (1 - 2 * bit_of(me, bit)) * (1 << bit)
    if bits >= 3 and bit == bits - 1:
        other = other + (1 - 2 * bit_of(me, bit - 1)) * (1 << (bit - 1))
    return other


def block_of(index, order):
    total = jnp.int32(0)
    for bit in order:
        total = total * 2 + coordinate(index, bit, len(order))
    return total


def device_of(block, order):
    bits = len(order)
    index = 0
    for place, bit in enumerate(reversed(order)):
        index += ((block >> place) & 1) << bit
    if bits >= 3 and (index >> (bits - 1)) & 1:
        index ^= 1 << (bits - 2)
    return index


def greet(me, bits, others=()):
    barrier = pltpu.get_barrier_semaphore()
    partners = [partner_of(me, bit, bits) for bit in range(bits)] + list(others)
    for partner in partners:
        pl.semaphore_signal(
            barrier,
            inc=1,
            device_id={"tok": partner},
            device_id_type=pl.DeviceIdType.MESH,
        )
    pl.semaphore_wait(barrier, len(partners))


def remote(src, dst, send_sem, recv_sem, partner):
    return pltpu.make_async_remote_copy(
        src_ref=src,
        dst_ref=dst,
        send_sem=send_sem,
        recv_sem=recv_sem,
        device_id={"tok": partner},
        device_id_type=pl.DeviceIdType.MESH,
    )


def gather_kernel(count, *refs):
    orders = axis_orders(count)
    bits = count.bit_length() - 1
    parts = refs[:3]
    q_ref, k_ref, v_ref, seg_col, seg_row = refs[3:8]
    outs, att_ref = refs[8:11], refs[11]
    held, old_k, old_v, old_seg, local_sem, send_sem, recv_sem, halo_send, halo_recv = refs[12:]
    me = lax.axis_index("tok")
    after, before = lax.rem(me + 1, count), lax.rem(me + count - 1, count)
    own = [block_of(me, orders[m]) for m in range(3)]
    local = [
        pltpu.make_async_copy(parts[m], held.at[m, own[m]], local_sem.at[m]) for m in range(3)
    ]
    for copy in local:
        copy.start()
    greet(me, bits, (after, before))
    copies = {}

    def send(m, step):
        bit = orders[m][bits - 1 - step]
        size = 1 << step
        start = lax.div(own[m], jnp.int32(size)) * size
        here = held.at[m, pl.ds(start, size)]
        copies[m, step] = remote(
            here, here, send_sem.at[m, step], recv_sem.at[m, step], partner_of(me, bit, bits)
        )
        copies[m, step].start()

    for m in range(3):
        local[m].wait()
        send(m, 0)
    halo = [
        remote(src, dst, halo_send.at[i], halo_recv.at[i], after)
        for i, (src, dst) in enumerate(((seg_row, old_seg), (k_ref, old_k), (v_ref, old_v)))
    ]
    for copy in halo:
        copy.start()

    rows = q_ref.shape[0]
    dim = D // ATT_HEADS
    scale = 1.0 / math.sqrt(dim)

    def attend_heads(first, last):
        row = lax.broadcasted_iota(jnp.int32, (rows, rows), 0)
        col = lax.broadcasted_iota(jnp.int32, (rows, rows), 1)
        own_seg = seg_col[...]
        now_ok = (col <= row) & (row - col < WINDOW) & (own_seg == seg_row[0:1, :])
        old_ok = (row - col + rows < WINDOW) & (own_seg == old_seg[0:1, :]) & (row + me * rows >= row + rows)

        def one(head, carry):
            lanes = pl.ds(pl.multiple_of(head * dim, dim), dim)
            q = q_ref[:, lanes]

            def score(keys, allowed):
                dots = lax.dot_general(
                    q, keys, (((1,), (1,)), ((), ())), preferred_element_type=jnp.float32
                )
                return jnp.where(allowed, dots * scale, jnp.float32(-1e30))

            old, now = score(old_k[:, lanes], old_ok), score(k_ref[:, lanes], now_ok)
            top = jnp.maximum(
                jnp.max(old, axis=1, keepdims=True), jnp.max(now, axis=1, keepdims=True)
            )
            old = jnp.where(old_ok, jnp.exp(old - top), jnp.float32(0.0))
            now = jnp.where(now_ok, jnp.exp(now - top), jnp.float32(0.0))
            total = jnp.sum(old, axis=1, keepdims=True) + jnp.sum(now, axis=1, keepdims=True)
            out = jnp.dot(
                (old / total).astype(jnp.bfloat16),
                old_v[:, lanes],
                preferred_element_type=jnp.float32,
            ) + jnp.dot(
                (now / total).astype(jnp.bfloat16),
                v_ref[:, lanes],
                preferred_element_type=jnp.float32,
            )
            att_ref[:, lanes] = out.astype(jnp.bfloat16)
            return carry

        lax.fori_loop(first, last, one, 0)

    for step in range(bits):
        if step == bits - 2:
            for copy in halo:
                copy.wait_recv()
            attend_heads(0, 6)
        if step == bits - 1:
            attend_heads(6, ATT_HEADS)
        for m in range(3):
            copies[m, step].wait_recv()
            if step + 1 < bits:
                send(m, step + 1)
            else:
                for block in range(count):
                    outs[m][device_of(block, orders[m])] = held[m, block]
    for copy in list(copies.values()) + halo:
        copy.wait_send()


def gather_weights(weights, queries, keys, values, segment, count):
    rows, cols = weights[0].shape
    tokens = queries.shape[0]
    bits = count.bit_length() - 1
    seg_row = jnp.broadcast_to(segment[None, :], (8, tokens))
    outs = pl.pallas_call(
        functools.partial(gather_kernel, count),
        out_shape=[jax.ShapeDtypeStruct((count, rows, cols), jnp.bfloat16)] * 3
        + [jax.ShapeDtypeStruct(queries.shape, jnp.bfloat16)],
        in_specs=[pl.BlockSpec(memory_space=pltpu.VMEM)] * 8,
        out_specs=[pl.BlockSpec(memory_space=pltpu.VMEM)] * 4,
        scratch_shapes=[
            pltpu.VMEM((3, count, rows, cols), jnp.bfloat16),
            pltpu.VMEM(keys.shape, jnp.bfloat16),
            pltpu.VMEM(values.shape, jnp.bfloat16),
            pltpu.VMEM((8, tokens), jnp.int32),
            pltpu.SemaphoreType.DMA((3,)),
            pltpu.SemaphoreType.DMA((3, bits)),
            pltpu.SemaphoreType.DMA((3, bits)),
            pltpu.SemaphoreType.DMA((3,)),
            pltpu.SemaphoreType.DMA((3,)),
        ],
        compiler_params=pltpu.CompilerParams(collective_id=0, has_side_effects=True),
        cost_estimate=pl.CostEstimate(flops=0, bytes_accessed=100_000_000, transcendentals=0),
    )(*weights, queries, keys, values, segment[:, None], seg_row)
    return [out.reshape(count * rows, cols) for out in outs[:3]], outs[3]


def update_kernel(count, *refs):
    orders = axis_orders(count)
    bits = count.bit_length() - 1
    hiddens, tokens = refs[:3], (refs[3], refs[3], refs[4])
    olds, outs = refs[5:8], refs[8:11]
    total, staged, landed, send_sem, recv_sem = refs[11:]
    rows, cols = olds[0].shape
    me = lax.axis_index("tok")
    own = [block_of(me, orders[m]) for m in range(3)]
    copies = {}

    def first_kept(m, step):
        size = count >> (step + 1)
        return lax.div(own[m], jnp.int32(size)) * size

    def half_start(m):
        return lax.div(own[m], jnp.int32(count // 2)) * (count // 2)

    def gradient(m, block, store):
        lead = count // 2 * rows
        chunk = 128
        each = chunk // rows
        lanes = pl.ds(pl.multiple_of(lax.div(block * rows, FAST_HID) * cols, cols), cols)
        wide = tokens[m][:, lanes]

        def one(i, carry):
            at = pl.ds(pl.multiple_of(block * rows + i * chunk, chunk), chunk)
            part = jnp.dot(hiddens[m][at, :], wide, preferred_element_type=jnp.float32)
            store(i * each, each, part.reshape(each, rows, cols))
            return carry

        lax.fori_loop(0, lead // chunk, one, 0)

    def stage_first(m, at, size, part):
        staged[m, pl.ds(at, size)] = part.astype(jnp.bfloat16)

    def keep_first(m, at, size, part):
        total[m, pl.ds(at, size)] = part

    def send_half(m, step):
        bit = orders[m][step]
        size = count >> (step + 1)
        place = pl.ds(count - 2 * size, size)
        copies[m, step] = remote(
            staged.at[m, place],
            landed.at[m, place],
            send_sem.at[m, step],
            recv_sem.at[m, step],
            partner_of(me, bit, bits),
        )
        copies[m, step].start()

    def pass_on(m, step):
        size = count >> (step + 1)
        base, keep = first_kept(m, step - 1), first_kept(m, step)
        away = 2 * base + size - keep
        half = half_start(m)
        below = count - 4 * size

        def sum_of(block):
            other = landed[m, below + block - base].astype(jnp.float32)
            return total[m, block - half] + other

        def stage(i, carry):
            staged[m, count - 2 * size + i] = sum_of(away + i).astype(jnp.bfloat16)
            return carry

        def hold(i, carry):
            total[m, keep - half + i] = sum_of(keep + i)
            return carry

        lax.fori_loop(0, size, stage, 0)
        send_half(m, step)
        lax.fori_loop(0, size, hold, 0)

    def send_new(m, step):
        bit = orders[m][bits - 1 - step]
        size = 1 << step
        start = lax.div(own[m], jnp.int32(size)) * size
        here = outs[m].at[pl.ds(start, size)]
        at = bits + step
        copies[m, at] = remote(
            here, here, send_sem.at[m, at], recv_sem.at[m, at], partner_of(me, bit, bits)
        )
        copies[m, at].start()

    for m in range(3):
        gradient(m, count // 2 - half_start(m), functools.partial(stage_first, m))
        if m == 0:
            greet(me, bits)
        send_half(m, 0)
    for m in range(3):
        gradient(m, half_start(m), functools.partial(keep_first, m))
    for step in range(1, bits):
        for m in range(3):
            copies[m, step - 1].wait_recv()
            pass_on(m, step)
    for m in range(3):
        copies[m, bits - 1].wait_recv()
        grad = total[m, own[m] - half_start(m)] + landed[m, count - 2].astype(jnp.float32)
        old = olds[m][...].astype(jnp.float32)
        update = old - grad
        old_len = jnp.sqrt(jnp.sum(old * old, axis=1, keepdims=True))
        new_len = jnp.sqrt(jnp.sum(update * update, axis=1, keepdims=True) + EPS)
        outs[m][own[m]] = (update * (old_len / new_len)).astype(jnp.bfloat16)
        send_new(m, 0)
    for step in range(bits):
        for m in range(3):
            copies[m, bits + step].wait_recv()
            if step + 1 < bits:
                send_new(m, step + 1)
    for copy in copies.values():
        copy.wait_send()


def update_weights(hiddens, keys, values, olds, count):
    rows, cols = olds[0].shape
    bits = count.bit_length() - 1
    shape = (count, rows, cols)
    return pl.pallas_call(
        functools.partial(update_kernel, count),
        out_shape=[jax.ShapeDtypeStruct(shape, jnp.bfloat16)] * 3,
        in_specs=[pl.BlockSpec(memory_space=pltpu.VMEM)] * 8,
        out_specs=[pl.BlockSpec(memory_space=pltpu.VMEM)] * 3,
        scratch_shapes=[
            pltpu.VMEM((3, count // 2, rows, cols), jnp.float32),
            pltpu.VMEM((3, count, rows, cols), jnp.bfloat16),
            pltpu.VMEM((3, count, rows, cols), jnp.bfloat16),
            pltpu.SemaphoreType.DMA((3, 2 * bits)),
            pltpu.SemaphoreType.DMA((3, 2 * bits)),
        ],
        compiler_params=pltpu.CompilerParams(collective_id=1, has_side_effects=True),
        cost_estimate=pl.CostEstimate(flops=0, bytes_accessed=200_000_000, transcendentals=0),
    )(*hiddens, keys, values, *olds)


def project(rows, weight):
    matrix = weight.reshape(FAST_HEADS, FAST_DIM, weight.shape[1])
    return jnp.einsum("thd,hdc->thc", rows, matrix, preferred_element_type=jnp.float32)


def hidden_first(hidden):
    return hidden.astype(jnp.bfloat16).reshape(hidden.shape[0], FAST_HEADS * FAST_HID).T


def per_device(queries, keys, values, segment, rates, fast_one, fast_three, fast_two):
    count = queries.shape[0]
    devices = lax.axis_size("tok")
    shard = lax.axis_index("tok")
    width = FAST_HEADS * FAST_DIM
    key_fast = keys.reshape(count, FAST_HEADS, FAST_DIM)
    value_fast = values.reshape(count, FAST_HEADS, FAST_DIM)
    query_fast = queries.reshape(count, FAST_HEADS, FAST_DIM)
    fulls, attended = gather_weights(
        (fast_one, fast_three, fast_two), queries, keys, values, segment, devices
    )
    full_one, full_three, full_two = fulls
    rate = rates[:, :, None]
    a_one = project(key_fast, full_one)
    a_three = project(key_fast, full_three)
    sig = jax.nn.sigmoid(a_one)
    weighted = (-rate * a_one * sig * a_three).astype(jnp.bfloat16)
    back = -rate * project(value_fast, full_two)
    delta_one = (back * a_three * sig * (1.0 + a_one * (1.0 - sig))).astype(jnp.bfloat16)
    delta_three = (back * a_one * sig).astype(jnp.bfloat16)
    hiddens = [hidden_first(hidden) for hidden in (delta_one, delta_three, weighted)]
    rows_here = FAST_HEADS * FAST_HID // devices
    olds = []
    for m, order in enumerate(axis_orders(devices)):
        start = block_of(shard, order) * rows_here
        own_cols = lax.dynamic_slice(
            fulls[m].reshape(FAST_HEADS, FAST_DIM, FAST_HID),
            (start // FAST_HID, jnp.int32(0), start % FAST_HID),
            (1, FAST_DIM, rows_here),
        )
        olds.append(own_cols[0].T)
    news = update_weights(hiddens, keys, values, olds, devices)
    new_one, new_three, new_two = [n.reshape(FAST_HEADS, FAST_HID, FAST_DIM) for n in news]
    b_one = jnp.einsum("thd,hcd->thc", query_fast, new_one, preferred_element_type=jnp.float32)
    b_three = jnp.einsum("thd,hcd->thc", query_fast, new_three, preferred_element_type=jnp.float32)
    mixed = (jax.nn.silu(b_one) * b_three).astype(jnp.bfloat16)
    fast_out = jnp.einsum("thc,hcd->thd", mixed, new_two, preferred_element_type=jnp.float32)
    fast_out = fast_out.reshape(count, width).astype(jnp.bfloat16)
    return (attended, fast_out)


def solution(mesh):
    placed = (
        P(("grp", "tok"), None),
        P(("grp", "tok"), None),
        P(("grp", "tok"), None),
        P(("grp", "tok")),
        P(("grp", "tok"), None),
        P(("grp", "tok"), None),
        P(("grp", "tok"), None),
        P(("grp", "tok"), None),
    )
    return jax.shard_map(
        per_device,
        mesh=mesh,
        in_specs=placed,
        out_specs=(P(("grp", "tok"), None), P(("grp", "tok"), None)),
        check_vma=False,
    )
```

time: 184 us -> 170 us (0.924)
  Pallas kernels: 137 us -> 147 us
  starting transfers between devices: 9.93 us -> 0 us
  matrix products: 21.1 us -> 11.2 us
  other arithmetic: 3.38 us -> 0.01 us
    ppermute x3 -> x0, starting transfers between devices: 9.93 us -> none  [from_behind(): lax.ppermute(value, axis, [(source, source + steps) for source in range(i...]
    dot_general x4 -> x0, matrix products: 8.2 us -> none  [the longest x3 6.17 us: outer_sum(): jnp.einsum('thc,thd->hcd', hidden, rows, preferred_element_type=jnp.float32)]
    pallas_call x1, Pallas kernels: 49.9 us -> 56.2 us  [gather_weights(): pl.pallas_call(functools.partial(gather_kernel, count), out_shape=[jax.Sh...]
    pallas_call x1, Pallas kernels: 87 us -> 90.7 us  [update_weights(): pl.pallas_call(functools.partial(update_kernel, count), out_shape=[jax.Sh...]
    broadcast_in_dim x0 -> x2, local copies, waits for them, and re-layouts: none -> 2.64 us  [the longest x1 1.39 us: gather_weights(): segment[:, None]]
    concatenate x3 -> x0, other arithmetic: 2.52 us -> none  [the longest x1 1.32 us: per_device(): all_keys = jnp.concatenate([prev_keys, keys], 0)]
    unnamed x18 -> x19, local copies, waits for them, and re-layouts: 7.11 us -> 4.67 us
    sub x1 -> x0, matrix products: 2.34 us -> none  [per_device(): expo = jnp.where(allowed[None], jnp.exp(masked - top), jnp.float32(0.0))]
  transfers between devices with their start and end apart: 3 -> 0, of which waited for: 0 -> 0; matrix products, arithmetic and copies ran while one was open for 15% -> 0% of each run, Pallas kernels for 75% -> 0%
where the time goes in v2:
time: 170 us
  Pallas kernels  147 us (86%)
  matrix products  11.2 us (7%)
  local copies, waits for them, and re-layouts  11 us (6%)
    pallas_call x1, Pallas kernels, update_weights(): pl.pallas_call(functools.partial(update_kernel, count), out_shape=[jax.Sh...  90.7 us
    pallas_call x1, Pallas kernels, gather_weights(): pl.pallas_call(functools.partial(gather_kernel, count), out_shape=[jax.Sh...  56.2 us
    dot_general x3, matrix products, project(): jnp.einsum('thd,hdc->thc', rows, matrix, preferred_element_type=jnp.float32)  5.35 us
    unnamed x19, local copies, waits for them, and re-layouts  4.67 us
    dot_general x1, matrix products, per_device(): jnp.einsum('thc,hcd->thd', mixed, new_two, preferred_element_type=jnp.flo...  3.6 us
    dynamic_slice x3, local copies, waits for them, and re-layouts, per_device(): lax.dynamic_slice(fulls[m].reshape(FAST_HEADS, FAST_DIM, FAST_HID), (star...  3.4 us

profile of v2, /device:TPU:0, one launch (start us, length us, event | category | flops | bytes accessed | tf_op | source)
XLA Modules:
  0.0 170.0 jit_solution(6605049891267202199)
XLA Ops:
  0.7 1.4 copy.10.refs_6_
  2.1 1.2 broadcast_in_dim.5.refs_7_
  3.4 56.2 %shard_map.95 = (bf16[32,64,512]{2,1,0:T(8,128)(2,1)}, bf16[32,64,512]{2,1,0:T(8,128)(2,1)}, bf16[32,64,512]{2,1,0:T(8,128)(2,1)}, bf16[128,2048]{1,0:T(8,128)(2,1)}) custom-call(bf16[64,512]{1,0:T(8,128)(2,1)} %refs_0_.1, bf16[64,512]{1,0:T(8,128)(2,1)} %refs_1_.1, bf16[64,512]{1,0:T(8,128)(2,1)} %refs_2_.1, bf16[128,2048]{1,0:T(8,128)(2,1)} %refs_3_.2, ...), custom_call_target="tpu_custom_call" | custom-call | bytes 100000000 | tf_op jit(solution)/shard_map/pallas_call | solution.py:191
  59.6 1.1 constant_dynamic-slice_fusion
  60.6 0.7 copy.32
  61.4 1.1 constant_dynamic-slice_fusion.1
  62.5 0.7 copy.31
  63.2 1.2 constant_dynamic-slice_fusion.2
  64.5 0.7 copy.30
  65.2 0.0 copy-done.6
  65.2 0.0 copy-done.1
  65.2 2.5 %fusion = f32[128,2,512]{0,2,1:T(8,128)S(1)} fusion(bf16[2,1024,512]{2,1,0:T(8,128)(2,1)} %bitcast.73, bf16[16,2,8,1024]{3,2,1,0:T(8,128)(2,1)S(1)} %bitcast.69, f32[128,2]{0,1:T(2,128)S(1)} %neg.12), kind=kOutput, calls=%fused_computation.6 | convolution fusion | flops 268566528 | bytes 3146752 | tf_op jit(solution)/shard_map/thd,hdc->thc/dot_general | solution.py:352
  67.7 0.0 copy-start.5
  67.8 0.0 copy-done
  67.8 0.0 copy-done.2
  67.8 0.9 convolution_bitcast_fusion.2
  68.7 0.6 copy-done.5
  69.3 1.9 %multiply_convert_fusion = (bf16[128,2,512]{0,2,1:T(8,128)(2,1)}, bf16[128,2,512]{0,2,1:T(8,128)(2,1)}, bf16[128,2,512]{0,2,1:T(8,128)(2,1)}) fusion(f32[128,2,512]{0,2,1:T(8,128)S(1)} %convolution_bitcast_fusion.2, f32[128,2]{0,1:T(2,128)S(1)} %neg.12, f32[128,2,512]{0,2,1:T(8,128)S(1)} %fusion, bf16[2,1024,512]{2,1,0:T(8,128)(2,1)S(1)} %bitcast.85, ...), kind=kOutput, calls=%fused_computation.18 | convolution fusion | flops 270663680 | bytes 4457472 | tf_op jit(solution)/shard_map/thd,hdc->thc/dot_general | solution.py:352
  71.2 90.7 %shard_map.96 = (bf16[32,32,1024]{2,1,0:T(8,128)(2,1)}, bf16[32,32,1024]{2,1,0:T(8,128)(2,1)}, bf16[32,32,1024]{2,1,0:T(8,128)(2,1)}) custom-call(bf16[1024,128]{1,0:T(8,128)(2,1)} %bitcast.82, bf16[1024,128]{1,0:T(8,128)(2,1)} %bitcast.83, bf16[1024,128]{1,0:T(8,128)(2,1)} %bitcast.81, bf16[128,2048]{1,0:T(8,128)(2,1)} %refs_3_.3, ...), custom_call_target="tpu_custom_call" | custom-call | bytes 200000000 | tf_op jit(solution)/shard_map/pallas_call | solution.py:333
  162.0 0.3 copy.33
  162.2 2.3 %convolution_bitcast_fusion.1 = f32[128,2,512]{0,2,1:T(8,128)S(1)} fusion(bf16[2,512,1024]{2,1,0:T(8,128)(2,1)} %bitcast.74, bf16[128,2,1024]{0,2,1:T(8,128)(2,1)S(1)} %bitcast.75), kind=kOutput, calls=%fused_computation.2 | convolution fusion | flops 268435456 | bytes 3145728 | tf_op jit(solution)/shard_map/thd,hcd->thc/dot_general | solution.py:392
  164.5 3.6 %convolution_convert_fusion = bf16[2,1024,128]{2,1,0:T(8,128)(2,1)S(1)} fusion(bf16[2,512,1024]{2,1,0:T(8,128)(2,1)} %bitcast.88, bf16[2,512,1024]{2,1,0:T(8,128)(2,1)} %bitcast.87, bf16[128,2,1024]{0,2,1:T(8,128)(2,1)S(1)} %bitcast.76, f32[128,2,512]{0,2,1:T(8,128)S(1)} %convolution_bitcast_fusion.1), kind=kOutput, calls=%fused_computation | convolution fusion | flops 537919488 | bytes 5767168 | tf_op jit(solution)/shard_map/thc,hcd->thd/dot_general | solution.py:395
  168.2 1.0 copy.23
  169.2 0.8 copy.51
  (9 shorter events, 0.0 us)
Async XLA Ops:
  3.4 61.9 %copy-start.6 = (f32[128,2]{0,1:T(2,128)S(1)}, f32[128,2]{0,1:T(2,128)}, u32[]{:S(2)}) copy-start(f32[128,2]{0,1:T(2,128)} %param.12) | copy-start | bytes 3076
  3.4 61.9 %copy-start.1 = (bf16[128,2048]{1,0:T(8,128)(2,1)S(1)}, bf16[128,2048]{1,0:T(8,128)(2,1)}, u32[]{:S(2)}) copy-start(bf16[128,2048]{1,0:T(8,128)(2,1)} %refs_4_.3) | copy-start | bytes 1572868
  63.2 4.5 %copy-start = (bf16[128,2048]{1,0:T(8,128)(2,1)S(1)}, bf16[128,2048]{1,0:T(8,128)(2,1)}, u32[]{:S(2)}) copy-start(bf16[128,2048]{1,0:T(8,128)(2,1)} %refs_3_.3) | copy-start | bytes 1572868
  63.2 4.5 %copy-start.2 = (bf16[32,64,512]{2,1,0:T(8,128)(2,1)S(1)}, bf16[32,64,512]{2,1,0:T(8,128)(2,1)}, u32[]{:S(2)}) copy-start(bf16[32,64,512]{2,1,0:T(8,128)(2,1)} %get-tuple-element.12) | copy-start | bytes 6291460
  67.7 1.6 copy-start.5
  71.2 90.7 %copy-start.3 = (bf16[128,2048]{1,0:T(8,128)(2,1)S(1)}, bf16[128,2048]{1,0:T(8,128)(2,1)}, u32[]{:S(2)}) copy-start(bf16[128,2048]{1,0:T(8,128)(2,1)} %refs_3_.2) | copy-start | bytes 1572868
  164.5 4.6 %copy-start.4 = (bf16[128,2048]{1,0:T(8,128)(2,1)S(1)}, bf16[128,2048]{1,0:T(8,128)(2,1)}, u32[]{:S(2)}) copy-start(bf16[128,2048]{1,0:T(8,128)(2,1)} %get-tuple-element.23) | copy-start | bytes 1572868

commit v3 on v2

--- a/solution.py
+++ b/solution.py
@@ -169,9 +169,9 @@
         if step == bits - 2:
             for copy in halo:
                 copy.wait_recv()
-            attend_heads(0, 6)
+            attend_heads(0, 12)
         if step == bits - 1:
-            attend_heads(6, ATT_HEADS)
+            attend_heads(12, ATT_HEADS)
         for m in range(3):
             copies[m, step].wait_recv()
             if step + 1 < bits:

time: 170 us -> 168 us (0.988)
  Pallas kernels: 147 us -> 144 us
    pallas_call x1, Pallas kernels: 90.7 us -> 88 us  [update_weights(): pl.pallas_call(functools.partial(update_kernel, count), out_shape=[jax.Sh...]
where the time goes in v3:
time: 168 us; the launch traced here: 167 us
  Pallas kernels  144 us (86%)
  matrix products  11.2 us (7%)
  local copies, waits for them, and re-layouts  11 us (7%)
    pallas_call x1, Pallas kernels, update_weights(): pl.pallas_call(functools.partial(update_kernel, count), out_shape=[jax.Sh...  88 us
    pallas_call x1, Pallas kernels, gather_weights(): pl.pallas_call(functools.partial(gather_kernel, count), out_shape=[jax.Sh...  56 us
    dot_general x3, matrix products, project(): jnp.einsum('thd,hdc->thc', rows, matrix, preferred_element_type=jnp.float32)  5.35 us
    unnamed x19, local copies, waits for them, and re-layouts  4.67 us
    dot_general x1, matrix products, per_device(): jnp.einsum('thc,hcd->thd', mixed, new_two, preferred_element_type=jnp.flo...  3.6 us
    dynamic_slice x3, local copies, waits for them, and re-layouts, per_device(): lax.dynamic_slice(fulls[m].reshape(FAST_HEADS, FAST_DIM, FAST_HID), (star...  3.4 us

profile of v3, /device:TPU:0, one launch (start us, length us, event | category | flops | bytes accessed | tf_op | source)
XLA Modules:
  0.0 167.0 jit_solution(3684442086085092469)
XLA Ops:
  0.7 1.4 copy.10.refs_6_
  2.1 1.2 broadcast_in_dim.5.refs_7_
  3.4 56.0 %shard_map.95 = (bf16[32,64,512]{2,1,0:T(8,128)(2,1)}, bf16[32,64,512]{2,1,0:T(8,128)(2,1)}, bf16[32,64,512]{2,1,0:T(8,128)(2,1)}, bf16[128,2048]{1,0:T(8,128)(2,1)}) custom-call(bf16[64,512]{1,0:T(8,128)(2,1)} %refs_0_.1, bf16[64,512]{1,0:T(8,128)(2,1)} %refs_1_.1, bf16[64,512]{1,0:T(8,128)(2,1)} %refs_2_.1, bf16[128,2048]{1,0:T(8,128)(2,1)} %refs_3_.2, ...), custom_call_target="tpu_custom_call" | custom-call | bytes 100000000 | tf_op jit(solution)/shard_map/pallas_call | solution.py:191
  59.3 1.1 constant_dynamic-slice_fusion
  60.4 0.7 copy.32
  61.2 1.1 constant_dynamic-slice_fusion.1
  62.3 0.7 copy.31
  63.0 1.2 constant_dynamic-slice_fusion.2
  64.3 0.7 copy.30
  65.0 0.0 copy-done.6
  65.0 0.0 copy-done.1
  65.0 2.5 %fusion = f32[128,2,512]{0,2,1:T(8,128)S(1)} fusion(bf16[2,1024,512]{2,1,0:T(8,128)(2,1)} %bitcast.73, bf16[16,2,8,1024]{3,2,1,0:T(8,128)(2,1)S(1)} %bitcast.69, f32[128,2]{0,1:T(2,128)S(1)} %neg.12), kind=kOutput, calls=%fused_computation.6 | convolution fusion | flops 268566528 | bytes 3146752 | tf_op jit(solution)/shard_map/thd,hdc->thc/dot_general | solution.py:352
  67.5 0.0 copy-start.5
  67.5 0.0 copy-done
  67.5 0.0 copy-done.2
  67.6 0.9 convolution_bitcast_fusion.2
  68.5 0.6 copy-done.5
  69.1 1.9 %multiply_convert_fusion = (bf16[128,2,512]{0,2,1:T(8,128)(2,1)}, bf16[128,2,512]{0,2,1:T(8,128)(2,1)}, bf16[128,2,512]{0,2,1:T(8,128)(2,1)}) fusion(f32[128,2,512]{0,2,1:T(8,128)S(1)} %convolution_bitcast_fusion.2, f32[128,2]{0,1:T(2,128)S(1)} %neg.12, f32[128,2,512]{0,2,1:T(8,128)S(1)} %fusion, bf16[2,1024,512]{2,1,0:T(8,128)(2,1)S(1)} %bitcast.85, ...), kind=kOutput, calls=%fused_computation.18 | convolution fusion | flops 270663680 | bytes 4457472 | tf_op jit(solution)/shard_map/thd,hdc->thc/dot_general | solution.py:352
  71.0 88.0 %shard_map.96 = (bf16[32,32,1024]{2,1,0:T(8,128)(2,1)}, bf16[32,32,1024]{2,1,0:T(8,128)(2,1)}, bf16[32,32,1024]{2,1,0:T(8,128)(2,1)}) custom-call(bf16[1024,128]{1,0:T(8,128)(2,1)} %bitcast.82, bf16[1024,128]{1,0:T(8,128)(2,1)} %bitcast.83, bf16[1024,128]{1,0:T(8,128)(2,1)} %bitcast.81, bf16[128,2048]{1,0:T(8,128)(2,1)} %refs_3_.3, ...), custom_call_target="tpu_custom_call" | custom-call | bytes 200000000 | tf_op jit(solution)/shard_map/pallas_call | solution.py:333
  159.0 0.3 copy.33
  159.3 2.3 %convolution_bitcast_fusion.1 = f32[128,2,512]{0,2,1:T(8,128)S(1)} fusion(bf16[2,512,1024]{2,1,0:T(8,128)(2,1)} %bitcast.74, bf16[128,2,1024]{0,2,1:T(8,128)(2,1)S(1)} %bitcast.75), kind=kOutput, calls=%fused_computation.2 | convolution fusion | flops 268435456 | bytes 3145728 | tf_op jit(solution)/shard_map/thd,hcd->thc/dot_general | solution.py:392
  161.6 3.6 %convolution_convert_fusion = bf16[2,1024,128]{2,1,0:T(8,128)(2,1)S(1)} fusion(bf16[2,512,1024]{2,1,0:T(8,128)(2,1)} %bitcast.88, bf16[2,512,1024]{2,1,0:T(8,128)(2,1)} %bitcast.87, bf16[128,2,1024]{0,2,1:T(8,128)(2,1)S(1)} %bitcast.76, f32[128,2,512]{0,2,1:T(8,128)S(1)} %convolution_bitcast_fusion.1), kind=kOutput, calls=%fused_computation | convolution fusion | flops 537919488 | bytes 5767168 | tf_op jit(solution)/shard_map/thc,hcd->thd/dot_general | solution.py:395
  165.2 1.0 copy.23
  166.2 0.8 copy.51
  (9 shorter events, 0.0 us)
Async XLA Ops:
  3.4 61.6 %copy-start.6 = (f32[128,2]{0,1:T(2,128)S(1)}, f32[128,2]{0,1:T(2,128)}, u32[]{:S(2)}) copy-start(f32[128,2]{0,1:T(2,128)} %param.12) | copy-start | bytes 3076
  3.4 61.7 %copy-start.1 = (bf16[128,2048]{1,0:T(8,128)(2,1)S(1)}, bf16[128,2048]{1,0:T(8,128)(2,1)}, u32[]{:S(2)}) copy-start(bf16[128,2048]{1,0:T(8,128)(2,1)} %refs_4_.3) | copy-start | bytes 1572868
  63.0 4.5 %copy-start = (bf16[128,2048]{1,0:T(8,128)(2,1)S(1)}, bf16[128,2048]{1,0:T(8,128)(2,1)}, u32[]{:S(2)}) copy-start(bf16[128,2048]{1,0:T(8,128)(2,1)} %refs_3_.3) | copy-start | bytes 1572868
  63.0 4.5 %copy-start.2 = (bf16[32,64,512]{2,1,0:T(8,128)(2,1)S(1)}, bf16[32,64,512]{2,1,0:T(8,128)(2,1)}, u32[]{:S(2)}) copy-start(bf16[32,64,512]{2,1,0:T(8,128)(2,1)} %get-tuple-element.12) | copy-start | bytes 6291460
  67.5 1.6 copy-start.5
  71.0 88.0 %copy-start.3 = (bf16[128,2048]{1,0:T(8,128)(2,1)S(1)}, bf16[128,2048]{1,0:T(8,128)(2,1)}, u32[]{:S(2)}) copy-start(bf16[128,2048]{1,0:T(8,128)(2,1)} %refs_3_.2) | copy-start | bytes 1572868
  161.6 4.6 %copy-start.4 = (bf16[128,2048]{1,0:T(8,128)(2,1)S(1)}, bf16[128,2048]{1,0:T(8,128)(2,1)}, u32[]{:S(2)}) copy-start(bf16[128,2048]{1,0:T(8,128)(2,1)} %get-tuple-element.23) | copy-start | bytes 1572868
